TPU v7x, 32 devices: a whole 2x2x4 slice. The times are simulated.
32 devices in a mesh: ta: 2 (over core), gx: 16 (over z, y, x).
Axes of the slice: x: 2, y: 2, z: 4, core: 2. Of those that a mesh axis runs over, the one named last changes fastest.
Arguments:
- time_links: float32 [6, 2, 3, 3, 96, 4608], P('ta', None, None, None, 'gx'), may hold values from -1 to 1, as said below
Outputs:
- loop_planes: float32 [96, 2, 4608], P('gx', None, 'ta')
- correlator: float32 [96, 49], P('gx')
Inputs may be any that keep to these rules, and one draw needn't show every extreme that they name: At every site and time, the matrix time_links[t, 0] + i time_links[t, 1] is special unitary.
All inputs are finite; a program needn't handle non-finite values.
Results may differ from a plain program's by a relative error of at most 0.00029.
Values sent between devices are 32-bit elements; how exact they have to be, the bound alone decides.
A program may use at most 64 MiB of HBM per device.

v0:
```python
import jax
import jax.numpy as jnp
from jax import lax
from jax.sharding import PartitionSpec as P


def prefix(value, axis, join, neutral):
    count, mine = (lax.axis_size(axis), lax.axis_index(axis))
    pieces = lax.all_gather(value, axis)
    subtotal = jnp.full_like(value, 0) + jnp.asarray(neutral, value.dtype)

    def step(position, subtotal):
        longer = join(subtotal, pieces[position])
        return jnp.where(position < mine, longer, subtotal)

    return lax.fori_loop(0, count - 1, step, subtotal)


def spread(value, axis, source):
    kept = jnp.where(lax.axis_index(axis) == source, value, 0).astype(value.dtype)
    return lax.psum(kept, axis)


def complex_mul(left, right):
    terms_real = []
    terms_imag = []
    for middle in range(3):
        left_real = left[0][:, middle : middle + 1]
        left_imag = left[1][:, middle : middle + 1]
        right_real = right[0][middle : middle + 1]
        right_imag = right[1][middle : middle + 1]
        terms_real.append(left_real * right_real - left_imag * right_imag)
        terms_imag.append(left_real * right_imag + left_imag * right_real)
    return jnp.stack(
        [
            terms_real[0] + terms_real[1] + terms_real[2],
            terms_imag[0] + terms_imag[1] + terms_imag[2],
        ]
    )


def trace_third(matrix):
    return (matrix[:, 0, 0] + matrix[:, 1, 1] + matrix[:, 2, 2]) / 3.0


def correlation(own_rows, others):
    return lax.dot_general(
        own_rows,
        others,
        (((1,), (1,)), ((), ())),
        precision=lax.Precision.HIGHEST,
        preferred_element_type=jnp.float32,
    )


def by_separation(products, offset, longest, period):
    row_index = lax.broadcasted_iota(jnp.int32, products.shape, 0)
    column_index = lax.broadcasted_iota(jnp.int32, products.shape, 1)
    separation = offset + column_index - row_index
    separation = separation % period
    targets = jnp.arange(longest + 1, dtype=jnp.int32)
    selector = (separation[:, :, None] == targets).astype(jnp.float32)
    return jnp.sum(products[:, :, None] * selector, axis=1)


def per_device(time_links):
    local_product = time_links[0]
    for slice_index in range(1, time_links.shape[0]):
        local_product = complex_mul(local_product, time_links[slice_index])
    plane_sites = time_links.shape[-1]
    ta_count = lax.axis_size("ta")
    site_share = plane_sites // ta_count
    unit_matrix = jnp.broadcast_to(
        jnp.eye(3, dtype=jnp.float32)[:, :, None, None], local_product.shape[1:]
    )
    identity = jnp.stack([unit_matrix, jnp.zeros_like(unit_matrix)])
    earlier = prefix(local_product, "ta", complex_mul, identity)
    full_product = complex_mul(earlier, local_product)
    traces = spread(trace_third(full_product), "ta", ta_count - 1)
    own_share = lax.dynamic_slice_in_dim(traces, lax.axis_index("ta") * site_share, site_share, 2)
    loop_planes = jnp.transpose(own_share, (1, 0, 2))
    planes = loop_planes.shape[0]
    flat_width = loop_planes.shape[1] * loop_planes.shape[2]
    gx_count = lax.axis_size("gx")
    far_blocks = gx_count // 2
    longest = planes * far_blocks
    own_rows = loop_planes.reshape(planes, flat_width)
    shard_rows = lax.all_gather(loop_planes, "gx", axis=0, tiled=True)
    products = correlation(own_rows, shard_rows.reshape(shard_rows.shape[0], flat_width))
    totals_part = by_separation(
        products, -lax.axis_index("gx") * planes, longest, planes * gx_count
    )
    correlator = lax.psum(totals_part, "ta") / plane_sites
    return (loop_planes, correlator)


def solution(mesh):
    in_specs = (P("ta", None, None, None, "gx", None),)
    out_specs = (P("gx", None, "ta"), P("gx", None))
    return jax.shard_map(
        per_device, mesh=mesh, in_specs=in_specs, out_specs=out_specs, check_vma=False
    )
```

profile of v0, /device:TPU:0, one launch (start us, length us, event | category | flops | bytes accessed | tf_op | source)
XLA Modules:
  0.0 143.7 jit_solution(14677089066934302279)
XLA Ops:
  7.2 5.7 %fusion.13 = (f32[1,1,1,3,6,4608]{5,1,4,3,2,0:T(1,128)S(1)}, f32[1,1,1,3,6,4608]{5,1,4,3,2,0:T(1,128)S(1)}, f32[1,1,1,3,6,4608]{5,1,4,3,2,0:T(1,128)S(1)}, f32[1...) fusion(f32[3,2,3,3,6,4608]{5,1,4,3,2,0:T(2,128)} %param.1), kind=kLoop, calls=%fused_computation.88 | loop fusion | bytes 7962624 | tf_op jit(solution)/shard_map/slice | solution.py:30
  12.9 3.9 %fusion.14 = (f32[1,1,3,3,6,4608]{5,1,4,3,2,0:T(1,128)S(1)}, f32[1,1,3,3,6,4608]{5,1,4,3,2,0:T(1,128)S(1)}) fusion(f32[3,2,3,3,6,4608]{5,1,4,3,2,0:T(2,128)} %param.1), kind=kLoop, calls=%fused_computation.89 | loop fusion | bytes 3981312 | tf_op jit(solution)/shard_map/slice | solution.py:28
  16.9 0.3 copy_bitcast_fusion
  17.4 0.1 copy_bitcast_fusion.8
  17.5 0.1 copy_bitcast_fusion.10
  17.8 1.0 subtract_add_fusion.4
  19.3 0.3 copy-done.1
  19.7 0.1 copy-done.2
  19.8 0.1 copy-done.3
  19.9 0.2 copy-done.4
  20.1 0.9 subtract_add_fusion.3
  21.0 1.8 %pad_maximum_fusion = f32[2,3,3,6,4608]{4,3,2,1,0:T(8,128)} fusion(f32[1,3,3,6,4608]{4,3,2,1,0:T(8,128)S(1)} %get-tuple-element.56, f32[1,3,3,6,4608]{4,3,2,1,0:T(8,128)S(1)} %get-tuple-element.55), kind=kLoop, calls=%fused_computation | loop fusion | flops 497664 | bytes 3981312 | tf_op jit(solution)/shard_map/stack | solution.py:34
  22.8 0.2 all-reduce.3.cloned.1.call-start
  23.1 2.4 %subtract_add_fusion.1 = (f32[3,3,6,4608]{3,2,1,0:T(8,128)S(1)}, f32[3,3,6,4608]{3,2,1,0:T(8,128)S(1)}) fusion(f32[3,6,4608]{2,1,0:T(8,128)S(1)} %get-tuple-element.90, f32[3,6,4608]{2,1,0:T(8,128)S(1)} %get-tuple-element.77, f32[3,6,4608]{2,1,0:T(8,128)S(1)} %get-tuple-element.91, f32[3,6,4608]{2,1,0:T(8,128)} %copy-done.3, ...), kind=kLoop, calls=%fused_computation.11 | loop fusion | flops 5474304 | bytes 5971968 | tf_op jit(solution)/shard_map/add | solution.py:36
  25.7 15.4 %all-gather.6.cloned.1.call-done = f32[4,3,3,6,4608]{4,3,2,1,0:T(8,128)} async-done(((f32[2,3,3,6,4608]{4,3,2,1,0:T(8,128)}), f32[4,3,3,6,4608]{4,3,2,1,0:T(8,128)}) %all-gather.6.cloned.1.call-update) | async-done | bytes 3981328 | tf_op jit(solution)/shard_map/all_gather | solution.py:9
  41.0 2.1 %broadcast_multiply_fusion.5 = (f32[3,6,4608]{2,1,0:T(8,128)S(1)}, f32[3,6,4608]{2,1,0:T(8,128)S(1)}, f32[3,6,4608]{2,1,0:T(8,128)S(1)}, f32[3,6,4608]{2,1,0:T(8...) fusion(f32[2,2,3,3,6,4608]{5,4,3,2,1,0:T(8,128)} %bitcast.118), kind=kLoop, calls=%fused_computation.72 | loop fusion | flops 497664 | bytes 3981312 | tf_op jit(solution)/shard_map/while/body/eval_jaxpr/mul | solution.py:32
  43.1 1.2 copy-done
  44.3 0.2 slice_bitcast_fusion.19
  44.5 0.9 subtract_add_fusion.2
  45.4 0.2 stack_broadcast_in_dim.2
  45.5 0.3 maximum_select_fusion
  45.9 0.2 slice_bitcast_fusion.1
  46.3 1.0 subtract_add_fusion
  47.2 0.8 fusion.8
  48.1 19.6 %all-reduce.3.cloned.1.call-done = f32[2,6,4608]{2,1,0:T(8,128)} async-done(((f32[2,6,4608]{2,1,0:T(8,128)}), f32[2,6,4608]{2,1,0:T(8,128)}) %all-reduce.3.cloned.1.call-update) | async-done | bytes 221200 | tf_op jit(solution)/shard_map/psum | solution.py:21
  67.7 0.9 dynamic-slice_bitcast_fusion
  68.6 0.7 copy.52
  69.3 61.6 %all-gather.4.cloned.1.call-done = f32[96,2,2304]{2,1,0:T(2,128)} async-done(((f32[6,2,2304]{2,1,0:T(2,128)}), f32[96,2,2304]{2,1,0:T(2,128)}) %all-gather.4.cloned.1.call-update) | async-done | bytes 1769488 | tf_op jit(solution)/shard_map/all_gather | solution.py:88
  131.0 2.9 %fusion.2 = f32[6,96]{1,0:T(8,128)S(1)} fusion(f32[6,2,2304]{2,0,1:T(8,128)S(1)} %dynamic-slice_bitcast_fusion, f32[96,2,2304]{2,1,0:T(2,128)} %all-gather.4.cloned.1.call-done), kind=kOutput, calls=%fused_computation.18 | convolution fusion | flops 31850496 | bytes 1882368 | tf_op jit(solution)/shard_map/dot_general | solution.py:47
  133.9 0.1 select_reduce_fusion
  134.1 2.5 %psum.15 = f32[6,49]{1,0:T(8,128)S(1)} all-reduce(f32[6,49]{1,0:T(8,128)S(1)} %select_reduce_fusion), channel_id=1, replica_groups=mesh['ta'=2,'gx'=16] {'ta'}, use_global_device_ids=true, to_apply=%region_2.3 | all-reduce | flops 294 | bytes 2352 | tf_op jit(solution)/shard_map/psum | solution.py:93
  136.5 0.6 broadcast_multiply_fusion.6
  (26 shorter events, 1.4 us)
Async XLA Ops:
  7.2 33.9 %all-gather.6.cloned.1.call-start = ((), (), s32[]{:S(2)}) async-start(), calls=%async_computation.2 | async-start | bytes 7962624 | tf_op jit(solution)/shard_map/all_gather | solution.py:9
  18.8 0.8 copy-start.1
  18.9 0.8 copy-start.2
  18.9 1.0 copy-start.3
  19.0 1.1 copy-start.4
  22.8 44.8 %all-reduce.3.cloned.1.call-start = ((), (), s32[]{:S(2)}) async-start(), calls=%async_computation | async-start | bytes 589824 | tf_op jit(solution)/shard_map/psum | solution.py:21
  41.0 3.3 %copy-start = (f32[4,3,3,6,4608]{4,3,2,1,0:T(8,128)S(1)}, f32[4,3,3,6,4608]{4,3,2,1,0:T(8,128)}, u32[]{:S(2)}) copy-start(f32[4,3,3,6,4608]{4,3,2,1,0:T(8,128)} %all-gather.6.cloned.1.call-done) | copy-start | bytes 11943940
  48.0 82.9 %all-gather.4.cloned.1.call-start = ((), (), s32[]{:S(2)}) async-start(), calls=%async_computation.1 | async-start | bytes 1880064 | tf_op jit(solution)/shard_map/all_gather | solution.py:88
Sparse Core Ops, SparseCore 0:
  22.9 18.0 all-gather.5
  48.2 19.4 all-reduce.2
  71.0 59.8 all-gather.3
where the time goes:
time: 144 us
  waiting for transfers between devices  96.6 us (67%)
  local copies, waits for them, and re-layouts  15.5 us (11%)
  between operations  14 us (10%)
  other arithmetic  11.8 us (8%)
  matrix products  2.94 us (2%)
  blocking collectives  2.47 us (2%)
    all_gather x1, waiting for transfers between devices, per_device(): shard_rows = lax.all_gather(loop_planes, 'gx', axis=0, tiled=True)  61.6 us
    psum x1, waiting for transfers between devices, spread(): return lax.psum(kept, axis)  19.6 us
    all_gather x1, waiting for transfers between devices, prefix(): pieces = lax.all_gather(value, axis)  15.4 us
    add x5, other arithmetic, complex_mul(): terms_real[0] + terms_real[1] + terms_real[2]  6.09 us
    slice x1, local copies, waits for them, and re-layouts, complex_mul(): right_real = right[0][middle:middle + 1]  5.72 us
    slice x2, local copies, waits for them, and re-layouts, complex_mul(): left_real = left[0][:, middle:middle + 1]  3.92 us
    dot_general x1, matrix products, correlation(): lax.dot_general(own_rows, others, (((1,), (1,)), ((), ())), precision=lax...  2.94 us
  transfers between devices with their start and end apart: 3, of which 3 were waited for; matrix products, arithmetic and copies ran while one was open for 2% of the time, Pallas kernels for 0%

commit v1 on v0

--- a/solution.py
+++ b/solution.py
@@ -85,7 +85,12 @@
     far_blocks = gx_count // 2
     longest = planes * far_blocks
     own_rows = loop_planes.reshape(planes, flat_width)
-    shard_rows = lax.all_gather(loop_planes, "gx", axis=0, tiled=True)
+    ring = [loop_planes]
+    for hop in range(15):
+        ring.append(lax.ppermute(ring[-1], "gx", [(dev, (dev + 1) % 16) for dev in range(16)]))
+    shard_rows = jnp.roll(
+        jnp.concatenate(ring[::-1], axis=0), (lax.axis_index("gx") + 1) * ring[0].shape[0], axis=0
+    )
     products = correlation(own_rows, shard_rows.reshape(shard_rows.shape[0], flat_width))
     totals_part = by_separation(
         products, -lax.axis_index("gx") * planes, longest, planes * gx_count

time: 144 us -> 271 us (1.88)
  waiting for transfers between devices: 96.6 us -> 167 us
  local copies, waits for them, and re-layouts: 15.5 us -> 68.8 us
    ppermute x0 -> x15, waiting for transfers between devices: none -> 132 us  [per_device(): lax.ppermute(ring[-1], 'gx', [(dev, (dev + 1) % 16) for dev in range(16)])]
    all_gather x1 -> x0, waiting for transfers between devices: 61.6 us -> none  [per_device(): shard_rows = lax.all_gather(loop_planes, 'gx', axis=0, tiled=True)]
    concatenate x0 -> x1, local copies, waits for them, and re-layouts: none -> 46.1 us  [per_device(): jnp.roll(jnp.concatenate(ring[::-1], axis=0), (lax.axis_index('gx') + 1)...]
    unnamed x11 -> x41, local copies, waits for them, and re-layouts: 2.65 us -> 9.87 us
  transfers between devices with their start and end apart: 3 -> 17, of which waited for: 3 -> 17; matrix products, arithmetic and copies ran while one was open for 2% -> 1% of each run, Pallas kernels for 0% -> 0%
where the time goes in v1:
time: 271 us; the launch traced here: 269 us
  waiting for transfers between devices  167 us (62%)
  local copies, waits for them, and re-layouts  68.8 us (25%)
  between operations  14.4 us (5%)
  other arithmetic  11.9 us (4%)
    ppermute x15, waiting for transfers between devices, per_device(): lax.ppermute(ring[-1], 'gx', [(dev, (dev + 1) % 16) for dev in range(16)])  132 us
    concatenate x1, local copies, waits for them, and re-layouts, per_device(): jnp.roll(jnp.concatenate(ring[::-1], axis=0), (lax.axis_index('gx') + 1)...  46.1 us
    psum x1, waiting for transfers between devices, spread(): return lax.psum(kept, axis)  19.6 us
    all_gather x1, waiting for transfers between devices, prefix(): pieces = lax.all_gather(value, axis)  15.4 us
    unnamed x41, local copies, waits for them, and re-layouts  9.87 us
    add x5, other arithmetic, complex_mul(): terms_real[0] + terms_real[1] + terms_real[2]  6.09 us
    slice x1, local copies, waits for them, and re-layouts, complex_mul(): right_real = right[0][middle:middle + 1]  5.72 us
  transfers between devices with their start and end apart: 17, of which 17 were waited for; matrix products, arithmetic and copies ran while one was open for 1% of the time, Pallas kernels for 0%

profile of v1, /device:TPU:0, one launch (start us, length us, event | category | flops | bytes accessed | tf_op | source)
XLA Modules:
  0.0 269.1 jit_solution(10334186285682721393)
XLA Ops:
  7.2 5.7 %fusion.14 = (f32[1,1,1,3,6,4608]{5,1,4,3,2,0:T(1,128)S(1)}, f32[1,1,1,3,6,4608]{5,1,4,3,2,0:T(1,128)S(1)}, f32[1,1,1,3,6,4608]{5,1,4,3,2,0:T(1,128)S(1)}, f32[1...) fusion(f32[3,2,3,3,6,4608]{5,1,4,3,2,0:T(2,128)} %param.1), kind=kLoop, calls=%fused_computation.89 | loop fusion | bytes 7962624 | tf_op jit(solution)/shard_map/slice | solution.py:30
  12.9 3.9 %fusion.15 = (f32[1,1,3,3,6,4608]{5,1,4,3,2,0:T(1,128)S(1)}, f32[1,1,3,3,6,4608]{5,1,4,3,2,0:T(1,128)S(1)}) fusion(f32[3,2,3,3,6,4608]{5,1,4,3,2,0:T(2,128)} %param.1), kind=kLoop, calls=%fused_computation.90 | loop fusion | bytes 3981312 | tf_op jit(solution)/shard_map/slice | solution.py:28
  17.8 1.0 subtract_add_fusion.4
  20.1 0.9 subtract_add_fusion.3
  21.0 1.8 pad_maximum_fusion
  23.1 2.4 subtract_add_fusion.1
  25.7 15.4 %all-gather.3.cloned.1.call-done = f32[4,3,3,6,4608]{4,3,2,1,0:T(8,128)} async-done(((f32[2,3,3,6,4608]{4,3,2,1,0:T(8,128)}), f32[4,3,3,6,4608]{4,3,2,1,0:T(8,128)}) %all-gather.3.cloned.1.call-update) | async-done | bytes 3981328 | tf_op jit(solution)/shard_map/all_gather | solution.py:9
  41.0 2.1 broadcast_multiply_fusion.5
  43.2 1.2 copy-done
  44.5 0.9 subtract_add_fusion.2
  46.3 1.0 subtract_add_fusion
  48.1 19.6 %all-reduce.3.cloned.1.call-done = f32[2,6,4608]{2,1,0:T(8,128)} async-done(((f32[2,6,4608]{2,1,0:T(8,128)}), f32[2,6,4608]{2,1,0:T(8,128)}) %all-reduce.3.cloned.1.call-update) | async-done | bytes 221200 | tf_op jit(solution)/shard_map/psum | solution.py:21
  67.7 0.9 dynamic-slice_bitcast_fusion
  68.6 1.8 collective-permute-start
  70.5 7.9 %collective-permute-done = f32[6,2,2304]{2,0,1:T(8,128)S(1)} collective-permute-done((f32[6,2,2304]{2,0,1:T(8,128)S(1)}, f32[6,2,2304]{2,0,1:T(8,128)S(1)}, u32[]{:S(2)}, u32[]{:S(2)}) %collective-permute-start) | collective-permute-done | bytes 110624 | tf_op jit(solution)/shard_map/ppermute | solution.py:90
  79.0 8.9 %collective-permute-done.1 = f32[6,2,2304]{2,0,1:T(8,128)S(1)} collective-permute-done((f32[6,2,2304]{2,0,1:T(8,128)S(1)}, f32[6,2,2304]{2,0,1:T(8,128)S(1)}, u32[]{:S(2)}, u32[]{:S(2)}) %collective-permute-start.1) | collective-permute-done | bytes 110624 | tf_op jit(solution)/shard_map/ppermute | solution.py:90
  88.6 8.7 %collective-permute-done.2 = f32[6,2,2304]{2,0,1:T(8,128)S(1)} collective-permute-done((f32[6,2,2304]{2,0,1:T(8,128)S(1)}, f32[6,2,2304]{2,0,1:T(8,128)S(1)}, u32[]{:S(2)}, u32[]{:S(2)}) %collective-permute-start.2) | collective-permute-done | bytes 110624 | tf_op jit(solution)/shard_map/ppermute | solution.py:90
  98.0 8.7 %collective-permute-done.3 = f32[6,2,2304]{2,0,1:T(8,128)S(1)} collective-permute-done((f32[6,2,2304]{2,0,1:T(8,128)S(1)}, f32[6,2,2304]{2,0,1:T(8,128)S(1)}, u32[]{:S(2)}, u32[]{:S(2)}) %collective-permute-start.3) | collective-permute-done | bytes 110624 | tf_op jit(solution)/shard_map/ppermute | solution.py:90
  107.4 8.7 %collective-permute-done.4 = f32[6,2,2304]{2,0,1:T(8,128)S(1)} collective-permute-done((f32[6,2,2304]{2,0,1:T(8,128)S(1)}, f32[6,2,2304]{2,0,1:T(8,128)S(1)}, u32[]{:S(2)}, u32[]{:S(2)}) %collective-permute-start.4) | collective-permute-done | bytes 110624 | tf_op jit(solution)/shard_map/ppermute | solution.py:90
  116.8 8.7 %collective-permute-done.5 = f32[6,2,2304]{2,0,1:T(8,128)S(1)} collective-permute-done((f32[6,2,2304]{2,0,1:T(8,128)S(1)}, f32[6,2,2304]{2,0,1:T(8,128)S(1)}, u32[]{:S(2)}, u32[]{:S(2)}) %collective-permute-start.5) | collective-permute-done | bytes 110624 | tf_op jit(solution)/shard_map/ppermute | solution.py:90
  126.2 9.0 %collective-permute-done.6 = f32[6,2,2304]{2,0,1:T(8,128)S(1)} collective-permute-done((f32[6,2,2304]{2,0,1:T(8,128)S(1)}, f32[6,2,2304]{2,0,1:T(8,128)S(1)}, u32[]{:S(2)}, u32[]{:S(2)}) %collective-permute-start.6) | collective-permute-done | bytes 110624 | tf_op jit(solution)/shard_map/ppermute | solution.py:90
  135.8 10.1 %collective-permute-done.7 = f32[6,2,2304]{2,0,1:T(8,128)S(1)} collective-permute-done((f32[6,2,2304]{2,0,1:T(8,128)S(1)}, f32[6,2,2304]{2,0,1:T(8,128)S(1)}, u32[]{:S(2)}, u32[]{:S(2)}) %collective-permute-start.7) | collective-permute-done | bytes 110624 | tf_op jit(solution)/shard_map/ppermute | solution.py:90
  146.6 9.4 %collective-permute-done.8 = f32[6,2,2304]{2,0,1:T(8,128)S(1)} collective-permute-done((f32[6,2,2304]{2,0,1:T(8,128)S(1)}, f32[6,2,2304]{2,0,1:T(8,128)S(1)}, u32[]{:S(2)}, u32[]{:S(2)}) %collective-permute-start.8) | collective-permute-done | bytes 110624 | tf_op jit(solution)/shard_map/ppermute | solution.py:90
  156.7 8.7 %collective-permute-done.9 = f32[6,2,2304]{2,0,1:T(8,128)S(1)} collective-permute-done((f32[6,2,2304]{2,0,1:T(8,128)S(1)}, f32[6,2,2304]{2,0,1:T(8,128)S(1)}, u32[]{:S(2)}, u32[]{:S(2)}) %collective-permute-start.9) | collective-permute-done | bytes 110624 | tf_op jit(solution)/shard_map/ppermute | solution.py:90
  166.1 8.7 %collective-permute-done.10 = f32[6,2,2304]{2,0,1:T(8,128)S(1)} collective-permute-done((f32[6,2,2304]{2,0,1:T(8,128)S(1)}, f32[6,2,2304]{2,0,1:T(8,128)S(1)}, u32[]{:S(2)}, u32[]{:S(2)}) %collective-permute-start.10) | collective-permute-done | bytes 110624 | tf_op jit(solution)/shard_map/ppermute | solution.py:90
  175.5 8.7 %collective-permute-done.11 = f32[6,2,2304]{2,0,1:T(8,128)S(1)} collective-permute-done((f32[6,2,2304]{2,0,1:T(8,128)S(1)}, f32[6,2,2304]{2,0,1:T(8,128)S(1)}, u32[]{:S(2)}, u32[]{:S(2)}) %collective-permute-start.11) | collective-permute-done | bytes 110624 | tf_op jit(solution)/shard_map/ppermute | solution.py:90
  184.2 8.7 %collective-permute-done.12 = f32[6,2,2304]{2,0,1:T(8,128)S(1)} collective-permute-done((f32[6,2,2304]{2,0,1:T(8,128)S(1)}, f32[6,2,2304]{2,0,1:T(8,128)S(1)}, u32[]{:S(2)}, u32[]{:S(2)}) %collective-permute-start.12) | collective-permute-done | bytes 110624 | tf_op jit(solution)/shard_map/ppermute | solution.py:90
  193.0 8.7 %collective-permute-done.13 = f32[6,2,2304]{2,0,1:T(8,128)S(1)} collective-permute-done((f32[6,2,2304]{2,0,1:T(8,128)S(1)}, f32[6,2,2304]{2,0,1:T(8,128)S(1)}, u32[]{:S(2)}, u32[]{:S(2)}) %collective-permute-start.13) | collective-permute-done | bytes 110624 | tf_op jit(solution)/shard_map/ppermute | solution.py:90
  202.5 8.1 %collective-permute-done.14 = f32[6,2,2304]{2,0,1:T(8,128)} collective-permute-done((f32[6,2,2304]{2,0,1:T(8,128)S(1)}, f32[6,2,2304]{2,0,1:T(8,128)}, u32[]{:S(2)}, u32[]{:S(2)}) %collective-permute-start.14) | collective-permute-done | bytes 110624 | tf_op jit(solution)/shard_map/ppermute | solution.py:90
  210.6 46.1 %concatenate.6 = f32[192,2,2304]{2,0,1:T(8,128)S(1)} concatenate(f32[6,2,2304]{2,0,1:T(8,128)} %collective-permute-done.14, f32[6,2,2304]{2,0,1:T(8,128)} %copy-done.19, f32[6,2,2304]{2,0,1:T(8,128)} %copy-done.18, f32[6,2,2304]{2,0,1:T(8,128)} %copy-done.17, f32[6,2,2304]{2,0,1:T(8,128)} %copy-done.16, f32[6,2,2304]{2,0,1:T(8,128)} %copy-done.15, f32[6,2,2304]{2,0,1:T(8,128)} %copy-done.14, ...), dimensions={0} | concatenate | bytes 7077888 | tf_op jit(solution)/shard_map/jit(_roll_dynamic)/concatenate | solution.py:91
  256.6 2.4 fusion.2
  259.2 2.5 psum.15
  (84 shorter events, 13.2 us)
Async XLA Ops:
  7.2 33.9 %all-gather.3.cloned.1.call-start = ((), (), s32[]{:S(2)}) async-start(), calls=%async_computation.1 | async-start | bytes 7962624 | tf_op jit(solution)/shard_map/all_gather | solution.py:9
  18.8 0.8 copy-start.1
  18.9 0.8 copy-start.2
  18.9 1.0 copy-start.3
  19.0 1.1 copy-start.4
  22.8 44.8 %all-reduce.3.cloned.1.call-start = ((), (), s32[]{:S(2)}) async-start(), calls=%async_computation | async-start | bytes 589824 | tf_op jit(solution)/shard_map/psum | solution.py:21
  41.0 3.3 %copy-start = (f32[4,3,3,6,4608]{4,3,2,1,0:T(8,128)S(1)}, f32[4,3,3,6,4608]{4,3,2,1,0:T(8,128)}, u32[]{:S(2)}) copy-start(f32[4,3,3,6,4608]{4,3,2,1,0:T(8,128)} %all-gather.3.cloned.1.call-done) | copy-start | bytes 11943940
  68.6 133.8 %copy-start.5 = (f32[6,2,2304]{2,0,1:T(8,128)}, f32[6,2,2304]{2,0,1:T(8,128)S(1)}, u32[]{:S(2)}) copy-start(f32[6,2,2304]{2,0,1:T(8,128)S(1)} %dynamic-slice_bitcast_fusion) | copy-start | bytes 331780
  68.6 9.8 %collective-permute-start = (f32[6,2,2304]{2,0,1:T(8,128)S(1)}, f32[6,2,2304]{2,0,1:T(8,128)S(1)}, u32[]{:S(2)}, u32[]{:S(2)}) collective-permute-start(f32[6,2,2304]{2,0,1:T(8,128)S(1)} %dynamic-slice_bitcast_fusion), channel_id=1, source_target_pairs={{0,1},{1,2},{2,3},{3,4},{4,5},{5,6},{6,7},{7,8},{8,9},{9,10},{10,1... | collective-permute-start | bytes 331784 | tf_op jit(solution)/shard_map/ppermute | solution.py:90
  79.0 8.9 %collective-permute-start.1 = (f32[6,2,2304]{2,0,1:T(8,128)S(1)}, f32[6,2,2304]{2,0,1:T(8,128)S(1)}, u32[]{:S(2)}, u32[]{:S(2)}) collective-permute-start(f32[6,2,2304]{2,0,1:T(8,128)S(1)} %collective-permute-done), channel_id=1, source_target_pairs={{0,1},{1,2},{2,3},{3,4},{4,5},{5,6},{6,7},{7,8},{8,9},{9,10},{10,1... | collective-permute-start | bytes 331784 | tf_op jit(solution)/shard_map/ppermute | solution.py:90
  87.9 0.7 copy-start.7
  88.6 8.7 %collective-permute-start.2 = (f32[6,2,2304]{2,0,1:T(8,128)S(1)}, f32[6,2,2304]{2,0,1:T(8,128)S(1)}, u32[]{:S(2)}, u32[]{:S(2)}) collective-permute-start(f32[6,2,2304]{2,0,1:T(8,128)S(1)} %collective-permute-done.1), channel_id=1, source_target_pairs={{0,1},{1,2},{2,3},{3,4},{4,5},{5,6},{6,7},{7,8},{8,9},{9,10},{10,1... | collective-permute-start | bytes 331784 | tf_op jit(solution)/shard_map/ppermute | solution.py:90
  97.3 0.7 copy-start.8
  98.0 8.7 %collective-permute-start.3 = (f32[6,2,2304]{2,0,1:T(8,128)S(1)}, f32[6,2,2304]{2,0,1:T(8,128)S(1)}, u32[]{:S(2)}, u32[]{:S(2)}) collective-permute-start(f32[6,2,2304]{2,0,1:T(8,128)S(1)} %collective-permute-done.2), channel_id=1, source_target_pairs={{0,1},{1,2},{2,3},{3,4},{4,5},{5,6},{6,7},{7,8},{8,9},{9,10},{10,1... | collective-permute-start | bytes 331784 | tf_op jit(solution)/shard_map/ppermute | solution.py:90
  106.7 0.7 copy-start.9
  107.4 8.7 %collective-permute-start.4 = (f32[6,2,2304]{2,0,1:T(8,128)S(1)}, f32[6,2,2304]{2,0,1:T(8,128)S(1)}, u32[]{:S(2)}, u32[]{:S(2)}) collective-permute-start(f32[6,2,2304]{2,0,1:T(8,128)S(1)} %collective-permute-done.3), channel_id=1, source_target_pairs={{0,1},{1,2},{2,3},{3,4},{4,5},{5,6},{6,7},{7,8},{8,9},{9,10},{10,1... | collective-permute-start | bytes 331784 | tf_op jit(solution)/shard_map/ppermute | solution.py:90
  116.8 8.7 %collective-permute-start.5 = (f32[6,2,2304]{2,0,1:T(8,128)S(1)}, f32[6,2,2304]{2,0,1:T(8,128)S(1)}, u32[]{:S(2)}, u32[]{:S(2)}) collective-permute-start(f32[6,2,2304]{2,0,1:T(8,128)S(1)} %collective-permute-done.4), channel_id=1, source_target_pairs={{0,1},{1,2},{2,3},{3,4},{4,5},{5,6},{6,7},{7,8},{8,9},{9,10},{10,1... | collective-permute-start | bytes 331784 | tf_op jit(solution)/shard_map/ppermute | solution.py:90
  125.5 0.7 copy-start.11
  126.2 9.0 %collective-permute-start.6 = (f32[6,2,2304]{2,0,1:T(8,128)S(1)}, f32[6,2,2304]{2,0,1:T(8,128)S(1)}, u32[]{:S(2)}, u32[]{:S(2)}) collective-permute-start(f32[6,2,2304]{2,0,1:T(8,128)S(1)} %collective-permute-done.5), channel_id=1, source_target_pairs={{0,1},{1,2},{2,3},{3,4},{4,5},{5,6},{6,7},{7,8},{8,9},{9,10},{10,1... | collective-permute-start | bytes 331784 | tf_op jit(solution)/shard_map/ppermute | solution.py:90
  135.8 10.1 %collective-permute-start.7 = (f32[6,2,2304]{2,0,1:T(8,128)S(1)}, f32[6,2,2304]{2,0,1:T(8,128)S(1)}, u32[]{:S(2)}, u32[]{:S(2)}) collective-permute-start(f32[6,2,2304]{2,0,1:T(8,128)S(1)} %collective-permute-done.6), channel_id=1, source_target_pairs={{0,1},{1,2},{2,3},{3,4},{4,5},{5,6},{6,7},{7,8},{8,9},{9,10},{10,1... | collective-permute-start | bytes 331784 | tf_op jit(solution)/shard_map/ppermute | solution.py:90
  145.9 0.7 copy-start.13
  146.6 9.4 %collective-permute-start.8 = (f32[6,2,2304]{2,0,1:T(8,128)S(1)}, f32[6,2,2304]{2,0,1:T(8,128)S(1)}, u32[]{:S(2)}, u32[]{:S(2)}) collective-permute-start(f32[6,2,2304]{2,0,1:T(8,128)S(1)} %collective-permute-done.7), channel_id=1, source_target_pairs={{0,1},{1,2},{2,3},{3,4},{4,5},{5,6},{6,7},{7,8},{8,9},{9,10},{10,1... | collective-permute-start | bytes 331784 | tf_op jit(solution)/shard_map/ppermute | solution.py:90
  156.7 8.7 %collective-permute-start.9 = (f32[6,2,2304]{2,0,1:T(8,128)S(1)}, f32[6,2,2304]{2,0,1:T(8,128)S(1)}, u32[]{:S(2)}, u32[]{:S(2)}) collective-permute-start(f32[6,2,2304]{2,0,1:T(8,128)S(1)} %collective-permute-done.8), channel_id=1, source_target_pairs={{0,1},{1,2},{2,3},{3,4},{4,5},{5,6},{6,7},{7,8},{8,9},{9,10},{10,1... | collective-permute-start | bytes 331784 | tf_op jit(solution)/shard_map/ppermute | solution.py:90
  166.1 8.7 %collective-permute-start.10 = (f32[6,2,2304]{2,0,1:T(8,128)S(1)}, f32[6,2,2304]{2,0,1:T(8,128)S(1)}, u32[]{:S(2)}, u32[]{:S(2)}) collective-permute-start(f32[6,2,2304]{2,0,1:T(8,128)S(1)} %collective-permute-done.9), channel_id=1, source_target_pairs={{0,1},{1,2},{2,3},{3,4},{4,5},{5,6},{6,7},{7,8},{8,9},{9,10},{10,1... | collective-permute-start | bytes 331784 | tf_op jit(solution)/shard_map/ppermute | solution.py:90
  174.8 0.7 copy-start.16
  175.5 8.7 %collective-permute-start.11 = (f32[6,2,2304]{2,0,1:T(8,128)S(1)}, f32[6,2,2304]{2,0,1:T(8,128)S(1)}, u32[]{:S(2)}, u32[]{:S(2)}) collective-permute-start(f32[6,2,2304]{2,0,1:T(8,128)S(1)} %collective-permute-done.10), channel_id=1, source_target_pairs={{0,1},{1,2},{2,3},{3,4},{4,5},{5,6},{6,7},{7,8},{8,9},{9,10},{10,1... | collective-permute-start | bytes 331784 | tf_op jit(solution)/shard_map/ppermute | solution.py:90
  184.2 18.2 %copy-start.17 = (f32[6,2,2304]{2,0,1:T(8,128)}, f32[6,2,2304]{2,0,1:T(8,128)S(1)}, u32[]{:S(2)}) copy-start(f32[6,2,2304]{2,0,1:T(8,128)S(1)} %collective-permute-done.11) | copy-start | bytes 331780
  184.2 8.7 %collective-permute-start.12 = (f32[6,2,2304]{2,0,1:T(8,128)S(1)}, f32[6,2,2304]{2,0,1:T(8,128)S(1)}, u32[]{:S(2)}, u32[]{:S(2)}) collective-permute-start(f32[6,2,2304]{2,0,1:T(8,128)S(1)} %collective-permute-done.11), channel_id=1, source_target_pairs={{0,1},{1,2},{2,3},{3,4},{4,5},{5,6},{6,7},{7,8},{8,9},{9,10},{10,1... | collective-permute-start | bytes 331784 | tf_op jit(solution)/shard_map/ppermute | solution.py:90
  193.0 9.5 %copy-start.18 = (f32[6,2,2304]{2,0,1:T(8,128)}, f32[6,2,2304]{2,0,1:T(8,128)S(1)}, u32[]{:S(2)}) copy-start(f32[6,2,2304]{2,0,1:T(8,128)S(1)} %collective-permute-done.12) | copy-start | bytes 331780
  193.0 8.7 %collective-permute-start.13 = (f32[6,2,2304]{2,0,1:T(8,128)S(1)}, f32[6,2,2304]{2,0,1:T(8,128)S(1)}, u32[]{:S(2)}, u32[]{:S(2)}) collective-permute-start(f32[6,2,2304]{2,0,1:T(8,128)S(1)} %collective-permute-done.12), channel_id=1, source_target_pairs={{0,1},{1,2},{2,3},{3,4},{4,5},{5,6},{6,7},{7,8},{8,9},{9,10},{10,1... | collective-permute-start | bytes 331784 | tf_op jit(solution)/shard_map/ppermute | solution.py:90
  201.7 0.8 copy-start.19
  201.7 8.8 %collective-permute-start.14 = (f32[6,2,2304]{2,0,1:T(8,128)S(1)}, f32[6,2,2304]{2,0,1:T(8,128)}, u32[]{:S(2)}, u32[]{:S(2)}) collective-permute-start(f32[6,2,2304]{2,0,1:T(8,128)S(1)} %collective-permute-done.13), channel_id=1, source_target_pairs={{0,1},{1,2},{2,3},{3,4},{4,5},{5,6},{6,7},{7,8},{8,9},{9,10},{10,1... | collective-permute-start | bytes 331784 | tf_op jit(solution)/shard_map/ppermute | solution.py:90
  (5 other events, 3.2 us)
Sparse Core Ops, SparseCore 0:
  23.0 18.0 all-gather.2
  48.2 19.4 all-reduce.2
